TPU v7x, 32 devices: a whole 2x2x4 slice. The times are simulated.
32 devices in a mesh: row: 4 (over x, core), col: 8 (over z, y).
Axes of the slice: x: 2, y: 2, z: 4, core: 2. Of those that a mesh axis runs over, the one named last changes fastest.
Arguments:
- tiles: bfloat16 [4, 8, 128, 128, 128], P('row', 'col')
- tile_row: int32 [4, 8, 128], P('row', 'col'), may hold values from 0 to 15, as said below
- tile_col: int32 [4, 8, 128], P('row', 'col'), may hold values from 0 to 15
- tile_count: int32 [4, 8], P('row', 'col'), may hold values from 1 to 128, as said below
- sinogram: float32 [4, 2048, 128], P('row', 'col')
Outputs:
- volume: float32 [8, 2048, 128], P('col', 'row')
- residual: float32 [4, 2048, 128], P('row', 'col')
Inputs may be any that keep to these rules, and one draw needn't show every extreme that they name: Within one block the pairs (tile_row, tile_col) of all 128 slots are distinct. Slots 0 to tile_count - 1 of a block are live, the rest are ignored; some block has all 128 slots live in every draw.
All inputs are finite; a program needn't handle non-finite values.
Results may differ from a plain program's by a relative error of at most 0.015.
Values may be sent and summed in bfloat16 or wider, within the bound.
A program may use at most 64 MiB of HBM per device.

v0:
```python
import functools

import jax
import jax.numpy as jnp
from jax import lax
from jax.experimental import pallas as pl
from jax.experimental.pallas import tpu as pltpu
from jax.sharding import PartitionSpec as P

RT = 16
VT = 16
ITERS = 4
CORES = 2
PIECE = 256
AXIS_REFS = 15
MESH = pl.DeviceIdType.MESH
F32 = jnp.float32
BF16 = jnp.bfloat16


def inner_size(n):
    size = 1
    while size * 2 * size * 2 <= n and n % (size * 2) == 0:
        size *= 2
    return size


def build(slot_ref, tiles, dense, flipped, start, stop):
    tile = tiles.shape[1]
    group = 4

    def place(step, carry):
        for j in range(group):
            at = step * group + j
            r = pl.multiple_of(at // VT * tile, tile)
            c = pl.multiple_of(lax.rem(at, VT) * tile, tile)
            block = tiles[slot_ref[at]]
            dense[pl.ds(r, tile), pl.ds(c, tile)] = block
            flipped[pl.ds(c, tile), pl.ds(r, tile)] = block.T
        return carry

    lax.fori_loop(start // group, stop // group, place, 0)


class Axis:
    def __init__(self, name, n, n_in, chunk, refs):
        self.name, self.n, self.n_in, self.n_out, self.chunk = name, n, n_in, n // n_in, chunk
        self.near_out, self.near_in, self.far_out, self.far_in, self.norm_in = refs[:5]
        (self.near_ss, self.near_rs, self.far_ss, self.far_rs, self.out_ss, self.out_rs,
         self.in_ss, self.in_rs, self.norm_ss, self.norm_rs) = refs[5:]
        self.me = lax.axis_index(name)
        self.o, self.i = self.me // n_in, lax.rem(self.me, n_in)

    def index(self, e, d):
        return lax.rem(self.o + e + self.n_out, self.n_out) * self.n_in + lax.rem(self.i + d + self.n_in, self.n_in)

    def rows(self, index):
        return pl.ds(pl.multiple_of(index * self.chunk, self.chunk), self.chunk)

    def send(self, src, dst, ss, rs, index):
        copy = pltpu.make_async_remote_copy(
            src_ref=src, dst_ref=dst, send_sem=ss, recv_sem=rs,
            device_id={self.name: index}, device_id_type=MESH,
        )
        copy.start()
        return copy

    def outer_order(self):
        return sorted(range(1, self.n_out), key=lambda e: -min(e, self.n_out - e)) + [0]

    def reduce_scatter(self, matrix, full, queued=lambda: None):
        def piece(index):
            return jnp.dot(matrix[self.rows(index), :], full[...], preferred_element_type=F32)

        copies = []
        near = {}
        for e in self.outer_order():
            for d in range(1, self.n_in):
                self.near_out[d - 1, e] = piece(self.index(e, d)).astype(BF16)
                near[e, d] = self.send(
                    self.near_out.at[d - 1, e], self.near_in.at[d - 1, e],
                    self.near_ss.at[d - 1, e], self.near_rs.at[d - 1, e], self.index(0, d))
        queued()
        far = {}
        total = None
        for e in self.outer_order():
            total = piece(self.index(e, 0))
            for d in range(1, self.n_in):
                near[e, d].wait_recv()
                total += self.near_in[d - 1, e].astype(F32)
            if e:
                self.far_out[e - 1] = total.astype(BF16)
                far[e] = self.send(
                    self.far_out.at[e - 1], self.far_in.at[e - 1],
                    self.far_ss.at[e - 1], self.far_rs.at[e - 1], self.index(e, 0))
        for e in far:
            far[e].wait_recv()
            total += self.far_in[e - 1].astype(F32)
        for copy in list(near.values()) + list(far.values()):
            copy.wait_send()
        return total

    def all_gather(self, value, full, between=lambda step: None):
        full[self.rows(self.me), :] = value.astype(BF16)
        mine = full.at[self.rows(self.me), :]
        far, near = {}, {}
        for e in reversed(self.outer_order()[:-1]):
            far[e] = self.send(mine, mine, self.out_ss.at[e - 1], self.out_rs.at[e - 1], self.index(e, 0))
        for d in range(1, self.n_in):
            near[0, d] = self.send(mine, mine, self.in_ss.at[d - 1, 0], self.in_rs.at[d - 1, 0], self.index(0, d))
        between(0)
        for step, e in enumerate(reversed(self.outer_order()[:-1])):
            far[e].wait_recv()
            theirs = full.at[self.rows(self.index(-e, 0)), :]
            for d in range(1, self.n_in):
                near[e, d] = self.send(
                    theirs, theirs, self.in_ss.at[d - 1, e], self.in_rs.at[d - 1, e], self.index(0, d))
            between(step + 1)
        for copy in near.values():
            copy.wait_recv()
        for copy in list(near.values()) + list(far.values()):
            copy.wait_send()

    def peer(self, d):
        return lax.rem(self.me + d, self.n)

    def norm_send(self, value, which):
        self.norm_in[which, 0] = jnp.broadcast_to(value, self.norm_in.shape[2:])
        return [
            self.send(self.norm_in.at[which, 0], self.norm_in.at[which, d],
                      self.norm_ss.at[which, d - 1], self.norm_rs.at[which, d - 1], self.peer(d))
            for d in range(1, self.n)
        ]

    def norm_wait(self, which):
        for d in range(1, self.n):
            pltpu.make_async_remote_copy(
                src_ref=self.norm_in.at[which, 0], dst_ref=self.norm_in.at[which, d],
                send_sem=self.norm_ss.at[which, d - 1], recv_sem=self.norm_rs.at[which, d - 1],
                device_id={self.name: self.peer(d)}, device_id_type=MESH,
            ).wait()
        total = self.norm_in[which, 0]
        for d in range(1, self.n):
            total += self.norm_in[which, d]
        return total[0:1, :]


class Exchange:
    def __init__(self, axis, pieces, refs):
        self.axis, self.pieces = axis, pieces
        self.near_out, self.near_in, self.far_out, self.far_in = refs[:4]
        self.near_ss, self.near_rs, self.far_ss, self.far_rs, self.back_ss, self.back_rs = refs[4:]

    def rows(self, core, at, size):
        chunk = self.axis.chunk
        start = (at // chunk * self.axis.n_in + core) * chunk + at % chunk
        return pl.ds(pl.multiple_of(start, size), size)

    def run(self, matrix, full, total, own):
        axis = self.axis
        mine, other = axis.i, 1 - axis.i
        near_peer, far_peer = axis.index(0, 1), axis.index(1, 0)

        def piece(core, at, size):
            return jnp.dot(matrix[self.rows(core, at, size), :], full[...], preferred_element_type=F32)

        def give(p):
            at, size = self.pieces[p]
            self.near_out[pl.ds(at, size)] = piece(other, at, size).astype(BF16)
            return axis.send(self.near_out.at[pl.ds(at, size)], self.near_in.at[pl.ds(at, size)],
                             self.near_ss.at[p], self.near_rs.at[p], near_peer)

        count = len(self.pieces)
        near, far, back = [give(0)], [], []
        for p, (at, size) in enumerate(self.pieces):
            if p + 1 < count:
                near.append(give(p + 1))
            part = piece(mine, at, size)
            near[p].wait_recv()
            here = pl.ds(at, size)
            self.far_out[here] = (part + self.near_in[here].astype(F32)).astype(BF16)
            far.append(axis.send(self.far_out.at[here], self.far_in.at[here],
                                 self.far_ss.at[p], self.far_rs.at[p], far_peer))
        for p, (at, size) in enumerate(self.pieces):
            far[p].wait_recv()
            here = pl.ds(at, size)
            rows = self.rows(mine, at, size)
            value = self.far_out[here].astype(F32) + self.far_in[here].astype(F32)
            total[rows] = value.astype(BF16)
            back.append(axis.send(total.at[rows], total.at[rows], self.back_ss.at[p], self.back_rs.at[p], near_peer))
        start = pl.multiple_of(axis.o * axis.chunk, axis.chunk)
        here = pl.ds(start, axis.chunk)
        own[...] = self.far_out[here].astype(F32) + self.far_in[here].astype(F32)
        for copy in back:
            copy.wait_recv()
        for copy in near + far + back:
            copy.wait_send()


def squares(ref, step):
    total = None
    for at in range(0, ref.shape[0], step):
        part = ref[at:at + step, :].astype(F32)
        part = jnp.sum(part * part, axis=0, keepdims=True)
        total = part if total is None else total + part
    return total


def cgls_kernel(sizes, slot_ref, tiles_hbm, sino_ref, volume_ref, residual_ref, tiles, dense, flipped, rays, voxels,
                images, held, search, direction, image, gamma, guess, load_sem, *refs):
    n_row, n_col, col_in, pieces = sizes
    row = Axis("row", n_row, CORES, search.shape[0], refs[:AXIS_REFS])
    col = Axis("col", n_col, col_in, image.shape[0], refs[AXIS_REFS:2 * AXIS_REFS])
    exchange = Exchange(row, pieces, refs[2 * AXIS_REFS:]) if pieces else None

    slots = tiles_hbm.shape[0]
    load = pltpu.make_async_copy(tiles_hbm, tiles.at[pl.ds(0, slots)], load_sem)
    load.start()
    tiles[slots] = jnp.zeros(tiles.shape[1:], tiles.dtype)

    barrier = pltpu.get_barrier_semaphore()
    for axis in (row, col):
        for d in range(1, axis.n):
            pl.semaphore_signal(barrier, inc=1, device_id={axis.name: axis.peer(d)}, device_id_type=MESH)
    pl.semaphore_wait(barrier, n_row + n_col - 2)

    share = RT * VT // col.n_out

    def build_share(step):
        if step == 0:
            load.wait()
        build(slot_ref, tiles, dense, flipped, step * share, (step + 1) * share)

    col.all_gather(sino_ref[...], rays, build_share)
    held[...] = rays[...].astype(F32)
    residual_ref[...] = sino_ref[...]
    volume_ref[...] = jnp.zeros_like(volume_ref)
    direction[...] = jnp.zeros_like(direction)
    image[...] = jnp.zeros_like(image)
    gamma[...] = jnp.ones_like(gamma)
    row.norm_send(squares(rays, 256), 1)

    def iteration(k, carry):
        if exchange:
            exchange.run(flipped, rays, voxels, search)
        else:
            search[...] = row.reduce_scatter(flipped, rays)
            row.all_gather(search[...], voxels)

        @pl.when(k == 0)
        def _():
            guess[...] = row.norm_wait(1)

        forth = col.reduce_scatter(dense, voxels, lambda: col.norm_send(squares(voxels, 256), 0))
        fresh = col.norm_wait(0)
        beta = jnp.where(k > 0, fresh / gamma[...], jnp.zeros_like(fresh))
        gamma[...] = fresh
        image[...] = forth + beta * image[...]
        col.norm_send(squares(image, image.shape[0]), 1)
        likely = jnp.where(k > 0, guess[...], guess[...] / fresh)

        @pl.when(k + 1 < ITERS)
        def _():
            def norm_on(step):
                if step == col.n_out - 1:
                    row.norm_send(col.norm_wait(1), 0)

            col.all_gather(residual_ref[...] - likely * image[...], images, norm_on)

        @pl.when(k + 1 == ITERS)
        def _():
            row.norm_send(col.norm_wait(1), 0)

        direction[...] = search[...] + beta * direction[...]
        alpha = fresh / row.norm_wait(0)
        guess[...] = 1.25 * alpha

        @pl.when(k + 1 < ITERS)
        def _():
            held[...] += alpha / likely * (images[...].astype(F32) - held[...])
            rays[...] = held[...].astype(BF16)

        residual_ref[...] -= alpha * image[...]
        volume_ref[...] += alpha * direction[...]
        return carry

    lax.fori_loop(0, ITERS, iteration, 0)


def axis_scratch(n, n_in, chunk, frames):
    n_out = n // n_in
    dma = pltpu.SemaphoreType.DMA
    near, far = (max(n_in - 1, 1), n_out), (max(n_out - 1, 1),)
    return [
        pltpu.VMEM(near + (chunk, frames), BF16),
        pltpu.VMEM(near + (chunk, frames), BF16),
        pltpu.VMEM(far + (chunk, frames), BF16),
        pltpu.VMEM(far + (chunk, frames), BF16),
        pltpu.VMEM((2, n, 8, frames), F32),
        dma(near), dma(near), dma(far), dma(far), dma(far), dma(far), dma(near), dma(near),
        dma((2, n - 1)), dma((2, n - 1)),
    ]


def exchange_scratch(count, rows, frames):
    buffer = pltpu.VMEM((rows, frames), BF16)
    return [buffer] * 4 + [pltpu.SemaphoreType.DMA((count,))] * 6


def local(n_row, n_col, tiles, tile_row, tile_col, tile_count, sinogram):
    tile, frames = tiles.shape[3], sinogram.shape[2]
    n_rays, n_vox = RT * tile, VT * tile
    vmem = pl.BlockSpec(memory_space=pltpu.VMEM)
    smem = pl.BlockSpec(memory_space=pltpu.SMEM)
    slots = tiles.shape[2]
    slot = jnp.arange(slots, dtype=jnp.int32)
    place = tile_row[0, 0] * VT + tile_col[0, 0]
    match = (place[None, :] == jnp.arange(RT * VT, dtype=jnp.int32)[:, None]) & (slot[None, :] < tile_count[0, 0])
    slot_of = jnp.min(jnp.where(match, slot[None, :], slots), axis=1)

    col_in = inner_size(n_col)
    vox_piece, ray_piece = n_vox // n_row, n_rays // n_col
    pieces = []
    if n_row == 2 * CORES:
        step = min(PIECE, vox_piece)
        pieces = [(at, step) for at in range(0, 2 * vox_piece, step)]
    hbm = pl.BlockSpec(memory_space=pl.ANY)
    volume, residual = pl.pallas_call(
        functools.partial(cgls_kernel, (n_row, n_col, col_in, pieces)),
        out_shape=(
            jax.ShapeDtypeStruct((vox_piece, frames), F32),
            jax.ShapeDtypeStruct((ray_piece, frames), F32),
        ),
        in_specs=[smem, hbm, vmem],
        out_specs=(vmem, vmem),
        scratch_shapes=[
            pltpu.VMEM((slots + 1, tile, tile), BF16),
            pltpu.VMEM((n_rays, n_vox), BF16),
            pltpu.VMEM((n_vox, n_rays), BF16),
            pltpu.VMEM((n_rays, frames), BF16),
            pltpu.VMEM((n_vox, frames), BF16),
            pltpu.VMEM((n_rays, frames), BF16),
            pltpu.VMEM((n_rays, frames), F32),
            pltpu.VMEM((vox_piece, frames), F32),
            pltpu.VMEM((vox_piece, frames), F32),
            pltpu.VMEM((ray_piece, frames), F32),
            pltpu.VMEM((1, frames), F32),
            pltpu.VMEM((1, frames), F32),
            pltpu.SemaphoreType.DMA,
        ]
        + axis_scratch(n_row, CORES, vox_piece, frames)
        + axis_scratch(n_col, col_in, ray_piece, frames)
        + (exchange_scratch(len(pieces), 2 * vox_piece, frames) if pieces else []),
        compiler_params=pltpu.CompilerParams(
            collective_id=0, has_side_effects=True, vmem_limit_bytes=62 * 1024 * 1024
        ),
        name="cgls",
    )(slot_of, tiles[0, 0], sinogram[0])
    return volume[None], residual[None]


def solution(mesh):
    return jax.shard_map(
        functools.partial(local, mesh.shape["row"], mesh.shape["col"]),
        mesh=mesh,
        in_specs=(
            P("row", "col", None, None, None),
            P("row", "col", None),
            P("row", "col", None),
            P("row", "col"),
            P("row", "col", None),
        ),
        out_specs=(P("col", "row", None), P("row", "col", None)),
        check_vma=False,
    )
```

profile of v0, /device:TPU:0, one launch (start us, length us, event | category | flops | bytes accessed | tf_op | source)
XLA Modules:
  0.0 158.2 jit_solution(13474038220085744383)
XLA Ops:
  1.3 0.7 add_bitcast_fusion
  2.0 0.7 select_reduce_fusion.slot_ref
  2.6 152.3 %cgls.1 = (f32[512,128]{1,0:T(8,128)}, f32[256,128]{1,0:T(8,128)}) custom-call(s32[256]{0:T(256)} %select_reduce_fusion.slot_ref, bf16[128,128,128]{2,1,0:T(8,128)(2,1)} %bitcast.8, f32[256,128]{1,0:T(8,128)} %bitcast.10), custom_call_target="tpu_custom_call" | custom-call | tf_op jit(solution)/shard_map/cgls/pallas_call | solution.py:328
  155.0 1.7 %copy.10 = f32[1,512,128]{2,1,0:T(8,128)} copy(f32[1,512,128]{2,1,0:T(8,128)} %bitcast.9) | data formatting | bytes 524288
  156.7 1.6 copy.11
  (1 shorter events, 0.0 us)
where the time goes:
time: 158 us
  Pallas kernels  152 us (96%)
  local copies, waits for them, and re-layouts  3.24 us (2%)
    pallas_call x1, Pallas kernels, local(): pl.pallas_call(functools.partial(cgls_kernel, (n_row, n_col, col_in, piec...  152 us
    unnamed x2, local copies, waits for them, and re-layouts  3.24 us

commit v1 on v0

--- a/solution.py
+++ b/solution.py
@@ -12,7 +12,9 @@
 ITERS = 4
 CORES = 2
 PIECE = 256
+PARTS = 2
 AXIS_REFS = 15
+LINE_REFS = 17
 MESH = pl.DeviceIdType.MESH
 F32 = jnp.float32
 BF16 = jnp.bfloat16
@@ -34,7 +36,7 @@
             at = step * group + j
             r = pl.multiple_of(at // VT * tile, tile)
             c = pl.multiple_of(lax.rem(at, VT) * tile, tile)
-            block = tiles[slot_ref[at]]
+            block = tiles[slot_ref[at // slot_ref.shape[2], 0, lax.rem(at, slot_ref.shape[2])]]
             dense[pl.ds(r, tile), pl.ds(c, tile)] = block
             flipped[pl.ds(c, tile), pl.ds(r, tile)] = block.T
         return carry
@@ -125,7 +127,7 @@
         return lax.rem(self.me + d, self.n)
 
     def norm_send(self, value, which):
-        self.norm_in[which, 0] = jnp.broadcast_to(value, self.norm_in.shape[2:])
+        self.norm_in[which, 0] = value
         return [
             self.send(self.norm_in.at[which, 0], self.norm_in.at[which, d],
                       self.norm_ss.at[which, d - 1], self.norm_rs.at[which, d - 1], self.peer(d))
@@ -142,7 +144,215 @@
         total = self.norm_in[which, 0]
         for d in range(1, self.n):
             total += self.norm_in[which, d]
-        return total[0:1, :]
+        return total
+
+
+class Line(Axis):
+    def __init__(self, name, n, n_in, chunk, refs):
+        self.near_out, self.near_in, self.far_out, self.far_in, self.norm_in, self.hold, self.total = refs[:7]
+        (self.near_ss, self.near_rs, self.far_ss, self.far_rs, self.out_ss, self.out_rs,
+         self.in_ss, self.in_rs, self.norm_ss, self.norm_rs) = refs[7:]
+        self.name, self.n, self.n_in, self.n_out, self.chunk = name, n, n_in, n // n_in, chunk
+        self.me = lax.axis_index(name)
+        self.o, self.i = self.me // n_in, lax.rem(self.me, n_in)
+        low = self.o < 2
+        self.edge = (self.o == 0) | (self.o == 3)
+        self.inner = jnp.logical_not(self.edge)
+        self.outer = [self.o, jnp.where(low, 1 - self.o, 5 - self.o), jnp.where(low, 2, 1), jnp.where(low, 3, 0)]
+        self.part = chunk // PARTS
+
+    def at(self, place, d=0):
+        return self.outer[place] * self.n_in + lax.rem(self.i + d, self.n_in)
+
+    def span(self, h):
+        return pl.ds(h * self.part, self.part)
+
+    def block(self, full, place, h):
+        start = pl.multiple_of(self.at(place) * self.chunk + h * self.part, self.part)
+        return full.at[pl.ds(start, self.part), :]
+
+    def link(self, src, dst, ss, rs, index):
+        return pltpu.make_async_remote_copy(
+            src_ref=src, dst_ref=dst, send_sem=ss, recv_sem=rs,
+            device_id={self.name: index}, device_id_type=MESH,
+        )
+
+    def reduce_scatter(self, matrix, full, queued=lambda: None):
+        def piece(index):
+            return jnp.dot(matrix[self.rows(index), :], full[...], preferred_element_type=F32)
+
+        parts, others = range(PARTS), range(1, self.n_in)
+        sent = []
+        for place in (3, 2, 1, 0):
+            for d in others:
+                self.near_out[d - 1, place] = piece(self.at(place, d)).astype(BF16)
+                for h in parts:
+                    copy = self.link(self.near_out.at[d - 1, place, self.span(h)],
+                                     self.near_in.at[d - 1, place, self.span(h)],
+                                     self.near_ss.at[d - 1, place, h], self.near_rs.at[d - 1, place, h],
+                                     self.at(0, d))
+                    copy.start()
+                    sent.append(copy)
+        queued()
+
+        def gathered(place, h):
+            part = self.hold[self.span(h)]
+            for d in others:
+                self.link(self.near_out.at[d - 1, place, self.span(h)], self.near_in.at[d - 1, place, self.span(h)],
+                          self.near_ss.at[d - 1, place, h], self.near_rs.at[d - 1, place, h],
+                          self.at(0, d)).wait_recv()
+                part += self.near_in[d - 1, place, self.span(h)].astype(F32)
+            return part
+
+        def far(which, slot, h, place):
+            return self.link(self.far_out.at[which, self.span(h)], self.far_in.at[slot, self.span(h)],
+                             self.far_ss.at[which, h], self.far_rs.at[slot, h], self.at(place))
+
+        self.hold[...] = piece(self.at(3))
+        for h in parts:
+            self.hold[self.span(h)] = gathered(3, h)
+
+            @pl.when(self.edge)
+            def _():
+                self.far_out[2, self.span(h)] = self.hold[self.span(h)].astype(BF16)
+                far(2, 3, h, 1).start()
+
+        self.total[...] = self.hold[...]
+        self.hold[...] = piece(self.at(2))
+        for h in parts:
+            self.far_out[1, self.span(h)] = gathered(2, h).astype(BF16)
+            far(1, jnp.where(self.edge, 2, 1), h, 2).start()
+        self.hold[...] = piece(self.at(1))
+
+        @pl.when(self.inner)
+        def _():
+            for h in parts:
+                far(2, 3, h, 1).wait_recv()
+                value = self.total[self.span(h)] + self.far_in[3, self.span(h)].astype(F32)
+                self.far_out[2, self.span(h)] = value.astype(BF16)
+                far(2, 1, h, 3).start()
+
+        for h in parts:
+            self.far_out[0, self.span(h)] = gathered(1, h).astype(BF16)
+            far(0, 0, h, 1).start()
+        self.hold[...] = piece(self.at(0))
+        for h in parts:
+            self.hold[self.span(h)] = gathered(0, h)
+        for h in parts:
+            far(0, 0, h, 1).wait_recv()
+            self.hold[self.span(h)] += self.far_in[0, self.span(h)].astype(F32)
+
+        @pl.when(self.inner)
+        def _():
+            for h in parts:
+                far(1, 2, h, 2).wait_recv()
+                self.hold[self.span(h)] += self.far_in[2, self.span(h)].astype(F32)
+
+        for h in parts:
+            far(1, 1, h, 2).wait_recv()
+            self.hold[self.span(h)] += self.far_in[1, self.span(h)].astype(F32)
+        for copy in sent:
+            copy.wait_send()
+        for which in range(3):
+            for h in parts:
+                far(which, 0, h, 1).wait_send()
+        return self.hold[...]
+
+    def all_gather(self, value, full, between=lambda step: None):
+        parts, others = range(PARTS), range(1, self.n_in)
+        full[self.rows(self.me), :] = value.astype(BF16)
+
+        def pass_on(place, slot, to, sem, h):
+            block = self.block(full, place, h)
+            return self.link(block, block, self.out_ss.at[sem, h], self.out_rs.at[slot - 1, h], self.at(to))
+
+        def arrived(place, h):
+            block = self.block(full, place, h)
+            self.link(block, block, self.out_ss.at[0, h], self.out_rs.at[place - 1, h], self.at(1)).wait_recv()
+
+        def share(place, h):
+            block = self.block(full, place, h)
+            return [self.link(block, block, self.in_ss.at[d - 1, place, h], self.in_rs.at[d - 1, place, h],
+                              self.at(0, d)) for d in others]
+
+        def spread(place, h):
+            for copy in share(place, h):
+                copy.start()
+
+        @pl.when(self.edge)
+        def _():
+            for h in parts:
+                pass_on(0, 3, 3, 0, h).start()
+            for h in parts:
+                pass_on(0, 1, 1, 2, h).start()
+                pass_on(0, 3, 2, 1, h).start()
+
+        @pl.when(self.inner)
+        def _():
+            for h in parts:
+                pass_on(0, 2, 2, 0, h).start()
+                pass_on(0, 1, 1, 1, h).start()
+
+        for h in parts:
+            spread(0, h)
+        between(0)
+
+        @pl.when(self.inner)
+        def _():
+            for h in parts:
+                arrived(2, h)
+                pass_on(2, 2, 1, 2, h).start()
+                spread(2, h)
+
+        for h in parts:
+            arrived(1, h)
+            spread(1, h)
+        between(1)
+        for h in parts:
+            arrived(3, h)
+            spread(3, h)
+        between(2)
+
+        @pl.when(self.edge)
+        def _():
+            for h in parts:
+                arrived(2, h)
+                spread(2, h)
+
+        between(3)
+        for place in range(4):
+            for h in parts:
+                for copy in share(place, h):
+                    copy.wait()
+        for sem in range(3):
+            for h in parts:
+                pass_on(0, 1, 1, sem, h).wait_send()
+
+
+class World:
+    def __init__(self, row, col, refs):
+        self.row, self.col = row, col
+        self.got, self.ss, self.rs = refs
+
+    def peers(self):
+        for at in range(1, self.row.n * self.col.n):
+            a, b = at // self.col.n, at % self.col.n
+            yield at, {self.row.name: self.row.peer(a), self.col.name: self.col.peer(b)}
+
+    def copy(self, at, device):
+        return pltpu.make_async_remote_copy(
+            src_ref=self.got.at[0], dst_ref=self.got.at[at], send_sem=self.ss.at[at - 1],
+            recv_sem=self.rs.at[at - 1], device_id=device, device_id_type=MESH)
+
+    def send(self, value):
+        self.got[0] = value
+        for at, device in self.peers():
+            self.copy(at, device).start()
+
+    def wait(self):
+        for at, device in self.peers():
+            self.copy(at, device).wait()
+        return jnp.sum(self.got[...], axis=0)
 
 
 class Exchange:
@@ -206,17 +416,30 @@
     return total
 
 
-def cgls_kernel(sizes, slot_ref, tiles_hbm, sino_ref, volume_ref, residual_ref, tiles, dense, flipped, rays, voxels,
-                images, held, search, direction, image, gamma, guess, load_sem, *refs):
+def cgls_kernel(sizes, count_ref, row_ref, col_ref, tiles_hbm, sino_ref, volume_ref, residual_ref, tiles, dense, flipped, rays, voxels,
+                images, held, search, direction, image, gamma, guess, ratio, load_sem, table, slot_ref, table_sem, *refs):
     n_row, n_col, col_in, pieces = sizes
     row = Axis("row", n_row, CORES, search.shape[0], refs[:AXIS_REFS])
-    col = Axis("col", n_col, col_in, image.shape[0], refs[AXIS_REFS:2 * AXIS_REFS])
-    exchange = Exchange(row, pieces, refs[2 * AXIS_REFS:]) if pieces else None
+    kind, count = (Line, LINE_REFS) if n_col == 4 * col_in else (Axis, AXIS_REFS)
+    col = kind("col", n_col, col_in, image.shape[0], refs[AXIS_REFS:AXIS_REFS + count])
+    refs = refs[AXIS_REFS + count:]
+    world = World(row, col, refs[:3])
+    exchange = Exchange(row, pieces, refs[3:]) if pieces else None
 
     slots = tiles_hbm.shape[0]
     load = pltpu.make_async_copy(tiles_hbm, tiles.at[pl.ds(0, slots)], load_sem)
     load.start()
     tiles[slots] = jnp.zeros(tiles.shape[1:], tiles.dtype)
+
+    place = (row_ref[...] * VT + col_ref[...]).astype(F32)
+    place = jnp.broadcast_to(place, (slots, slots)).T
+    slot = lax.broadcasted_iota(jnp.int32, (slots, slots), 0)
+    lane = lax.broadcasted_iota(jnp.int32, (slots, slots), 1).astype(F32)
+    for at in range(0, RT * VT, slots):
+        live = (place == lane + at) & (slot < count_ref[...])
+        table[at // slots] = jnp.min(jnp.where(live, slot, slots), axis=0, keepdims=True)
+    fill = pltpu.make_async_copy(table, slot_ref, table_sem)
+    fill.start()
 
     barrier = pltpu.get_barrier_semaphore()
     for axis in (row, col):
@@ -229,6 +452,7 @@
     def build_share(step):
         if step == 0:
             load.wait()
+            fill.wait()
         build(slot_ref, tiles, dense, flipped, step * share, (step + 1) * share)
 
     col.all_gather(sino_ref[...], rays, build_share)
@@ -256,32 +480,30 @@
         beta = jnp.where(k > 0, fresh / gamma[...], jnp.zeros_like(fresh))
         gamma[...] = fresh
         image[...] = forth + beta * image[...]
-        col.norm_send(squares(image, image.shape[0]), 1)
         likely = jnp.where(k > 0, guess[...], guess[...] / fresh)
 
+        def start(step):
+            if step == 0:
+                world.send(squares(image, image.shape[0]))
+                direction[...] = search[...] + beta * direction[...]
+            if step == col.n_out - 1:
+                alpha = fresh / world.wait()
+                guess[...] = 1.25 * alpha
+                ratio[...] = alpha / likely
+                residual_ref[...] -= alpha * image[...]
+                volume_ref[...] += alpha * direction[...]
+
         @pl.when(k + 1 < ITERS)
         def _():
-            def norm_on(step):
-                if step == col.n_out - 1:
-                    row.norm_send(col.norm_wait(1), 0)
-
-            col.all_gather(residual_ref[...] - likely * image[...], images, norm_on)
+            col.all_gather(residual_ref[...] - likely * image[...], images, start)
+            held[...] += ratio[...] * (images[...].astype(F32) - held[...])
+            rays[...] = held[...].astype(BF16)
 
         @pl.when(k + 1 == ITERS)
         def _():
-            row.norm_send(col.norm_wait(1), 0)
-
-        direction[...] = search[...] + beta * direction[...]
-        alpha = fresh / row.norm_wait(0)
-        guess[...] = 1.25 * alpha
-
-        @pl.when(k + 1 < ITERS)
-        def _():
-            held[...] += alpha / likely * (images[...].astype(F32) - held[...])
-            rays[...] = held[...].astype(BF16)
-
-        residual_ref[...] -= alpha * image[...]
-        volume_ref[...] += alpha * direction[...]
+            for step in range(col.n_out):
+                start(step)
+
         return carry
 
     lax.fori_loop(0, ITERS, iteration, 0)
@@ -296,15 +518,41 @@
         pltpu.VMEM(near + (chunk, frames), BF16),
         pltpu.VMEM(far + (chunk, frames), BF16),
         pltpu.VMEM(far + (chunk, frames), BF16),
-        pltpu.VMEM((2, n, 8, frames), F32),
+        pltpu.VMEM((2, n, 1, frames), F32),
         dma(near), dma(near), dma(far), dma(far), dma(far), dma(far), dma(near), dma(near),
         dma((2, n - 1)), dma((2, n - 1)),
     ]
 
 
+def line_scratch(n, n_in, chunk, frames):
+    dma = pltpu.SemaphoreType.DMA
+    near = (max(n_in - 1, 1), 4)
+    return [
+        pltpu.VMEM(near + (chunk, frames), BF16),
+        pltpu.VMEM(near + (chunk, frames), BF16),
+        pltpu.VMEM((3, chunk, frames), BF16),
+        pltpu.VMEM((4, chunk, frames), BF16),
+        pltpu.VMEM((2, n, 1, frames), F32),
+        pltpu.VMEM((chunk, frames), F32),
+        pltpu.VMEM((chunk, frames), F32),
+        dma(near + (PARTS,)), dma(near + (PARTS,)), dma((3, PARTS)), dma((4, PARTS)),
+        dma((3, PARTS)), dma((3, PARTS)), dma(near + (PARTS,)), dma(near + (PARTS,)),
+        dma((2, n - 1)), dma((2, n - 1)),
+    ]
+
+
 def exchange_scratch(count, rows, frames):
     buffer = pltpu.VMEM((rows, frames), BF16)
     return [buffer] * 4 + [pltpu.SemaphoreType.DMA((count,))] * 6
+
+
+def finish(volume_ref, residual_ref, volume_out, residual_out, sems):
+    copies = [pltpu.make_async_copy(volume_ref, volume_out, sems.at[0]),
+              pltpu.make_async_copy(residual_ref, residual_out, sems.at[1])]
+    for copy in copies:
+        copy.start()
+    for copy in copies:
+        copy.wait()
 
 
 def local(n_row, n_col, tiles, tile_row, tile_col, tile_count, sinogram):
@@ -313,11 +561,6 @@
     vmem = pl.BlockSpec(memory_space=pltpu.VMEM)
     smem = pl.BlockSpec(memory_space=pltpu.SMEM)
     slots = tiles.shape[2]
-    slot = jnp.arange(slots, dtype=jnp.int32)
-    place = tile_row[0, 0] * VT + tile_col[0, 0]
-    match = (place[None, :] == jnp.arange(RT * VT, dtype=jnp.int32)[:, None]) & (slot[None, :] < tile_count[0, 0])
-    slot_of = jnp.min(jnp.where(match, slot[None, :], slots), axis=1)
-
     col_in = inner_size(n_col)
     vox_piece, ray_piece = n_vox // n_row, n_rays // n_col
     pieces = []
@@ -331,7 +574,7 @@
             jax.ShapeDtypeStruct((vox_piece, frames), F32),
             jax.ShapeDtypeStruct((ray_piece, frames), F32),
         ),
-        in_specs=[smem, hbm, vmem],
+        in_specs=[vmem, vmem, vmem, hbm, vmem],
         out_specs=(vmem, vmem),
         scratch_shapes=[
             pltpu.VMEM((slots + 1, tile, tile), BF16),
@@ -346,16 +589,32 @@
             pltpu.VMEM((ray_piece, frames), F32),
             pltpu.VMEM((1, frames), F32),
             pltpu.VMEM((1, frames), F32),
+            pltpu.VMEM((1, frames), F32),
+            pltpu.SemaphoreType.DMA,
+            pltpu.VMEM((RT * VT // slots, 1, slots), jnp.int32),
+            pltpu.SMEM((RT * VT // slots, 1, slots), jnp.int32),
             pltpu.SemaphoreType.DMA,
         ]
         + axis_scratch(n_row, CORES, vox_piece, frames)
-        + axis_scratch(n_col, col_in, ray_piece, frames)
+        + (line_scratch if n_col == 4 * col_in else axis_scratch)(n_col, col_in, ray_piece, frames)
+        + [pltpu.VMEM((n_row * n_col, 1, frames), F32)] + [pltpu.SemaphoreType.DMA((n_row * n_col - 1,))] * 2
         + (exchange_scratch(len(pieces), 2 * vox_piece, frames) if pieces else []),
         compiler_params=pltpu.CompilerParams(
             collective_id=0, has_side_effects=True, vmem_limit_bytes=62 * 1024 * 1024
         ),
         name="cgls",
-    )(slot_of, tiles[0, 0], sinogram[0])
+    )(tile_count, tile_row[0], tile_col[0], tiles[0, 0], sinogram[0])
+    volume, residual = pl.pallas_call(
+        finish,
+        out_shape=(
+            jax.ShapeDtypeStruct((vox_piece, frames), F32),
+            jax.ShapeDtypeStruct((ray_piece, frames), F32),
+        ),
+        in_specs=[vmem, vmem],
+        out_specs=(hbm, hbm),
+        scratch_shapes=[pltpu.SemaphoreType.DMA((2,))],
+        name="finish",
+    )(volume, residual)
     return volume[None], residual[None]
 
 

time: 158 us -> 146 us (0.924)
  Pallas kernels: 152 us -> 145 us
  local copies, waits for them, and re-layouts: 3.24 us -> 0 us
    pallas_call x1, Pallas kernels: 152 us -> 143 us  [local(): pl.pallas_call(functools.partial(cgls_kernel, (n_row, n_col, col_in, piec...]
    unnamed x2 -> x0, local copies, waits for them, and re-layouts: 3.24 us -> none
    pallas_call x0 -> x1, Pallas kernels: none -> 1.74 us  [local(): pl.pallas_call(finish, out_shape=(jax.ShapeDtypeStruct((vox_piece, frames...]
where the time goes in v1:
time: 146 us
  Pallas kernels  145 us (99%)
    pallas_call x1, Pallas kernels, local(): pl.pallas_call(functools.partial(cgls_kernel, (n_row, n_col, col_in, piec...  143 us

profile of v1, /device:TPU:0, one launch (start us, length us, event | category | flops | bytes accessed | tf_op | source)
XLA Modules:
  0.0 146.1 jit_solution(3138293316987041999)
XLA Ops:
  1.3 143.1 %cgls.1 = (f32[512,128]{1,0:T(8,128)}, f32[256,128]{1,0:T(8,128)}) custom-call(s32[1,1]{1,0:T(1,128)S(6)} %copy.7.count_ref, s32[1,128]{1,0:T(1,128)} %bitcast.8, s32[1,128]{1,0:T(1,128)} %bitcast.9, bf16[128,128,128]{2,1,0:T(8,128)(2,1)} %bitcast.6, f32[256,128]{1,0:T(8,128)} %bitcast.7), custom_call_target="tpu_custom_call" | custom-call | tf_op jit(solution)/shard_map/cgls/pallas_call | solution.py:571
  144.4 1.7 %finish.1 = (f32[512,128]{1,0:T(8,128)}, f32[256,128]{1,0:T(8,128)}) custom-call(f32[512,128]{1,0:T(8,128)} %get-tuple-element.6.volume_ref, f32[256,128]{1,0:T(8,128)} %get-tuple-element.7.residual_ref), custom_call_target="tpu_custom_call" | custom-call | tf_op jit(solution)/shard_map/finish/pallas_call | solution.py:607

commit v2 on v1

--- a/solution.py
+++ b/solution.py
@@ -12,7 +12,7 @@
 ITERS = 4
 CORES = 2
 PIECE = 256
-PARTS = 2
+PARTS = 4
 AXIS_REFS = 15
 LINE_REFS = 17
 MESH = pl.DeviceIdType.MESH
@@ -102,7 +102,7 @@
             copy.wait_send()
         return total
 
-    def all_gather(self, value, full, between=lambda step: None):
+    def all_gather(self, value, full, between=lambda step: None, use=lambda rows: None):
         full[self.rows(self.me), :] = value.astype(BF16)
         mine = full.at[self.rows(self.me), :]
         far, near = {}, {}
@@ -120,6 +120,8 @@
             between(step + 1)
         for copy in near.values():
             copy.wait_recv()
+        for index in range(self.n):
+            use(self.rows(index))
         for copy in list(near.values()) + list(far.values()):
             copy.wait_send()
 
@@ -258,7 +260,7 @@
                 far(which, 0, h, 1).wait_send()
         return self.hold[...]
 
-    def all_gather(self, value, full, between=lambda step: None):
+    def all_gather(self, value, full, between=lambda step: None, use=lambda rows: None):
         parts, others = range(PARTS), range(1, self.n_in)
         full[self.rows(self.me), :] = value.astype(BF16)
 
@@ -321,9 +323,13 @@
 
         between(3)
         for place in range(4):
+            use(self.rows(self.at(place)))
+        for place in (0, 1, 3, 2):
             for h in parts:
                 for copy in share(place, h):
                     copy.wait()
+            for d in others:
+                use(self.rows(self.at(place, d)))
         for sem in range(3):
             for h in parts:
                 pass_on(0, 1, 1, sem, h).wait_send()
@@ -403,8 +409,12 @@
         own[...] = self.far_out[here].astype(F32) + self.far_in[here].astype(F32)
         for copy in back:
             copy.wait_recv()
-        for copy in near + far + back:
-            copy.wait_send()
+
+        def settle():
+            for copy in near + far + back:
+                copy.wait_send()
+
+        return settle
 
 
 def squares(ref, step):
@@ -416,8 +426,9 @@
     return total
 
 
-def cgls_kernel(sizes, count_ref, row_ref, col_ref, tiles_hbm, sino_ref, volume_ref, residual_ref, tiles, dense, flipped, rays, voxels,
-                images, held, search, direction, image, gamma, guess, ratio, load_sem, table, slot_ref, table_sem, *refs):
+def cgls_kernel(sizes, count_hbm, row_hbm, col_hbm, tiles_hbm, sino_hbm, volume_ref, residual_ref, tiles, dense, flipped, rays, voxels,
+                images, held, search, direction, image, gamma, guess, ratio, load_sem, table, slot_ref, table_sem,
+                count_ref, row_ref, col_ref, sino_ref, bring_sems, *refs):
     n_row, n_col, col_in, pieces = sizes
     row = Axis("row", n_row, CORES, search.shape[0], refs[:AXIS_REFS])
     kind, count = (Line, LINE_REFS) if n_col == 4 * col_in else (Axis, AXIS_REFS)
@@ -426,9 +437,19 @@
     world = World(row, col, refs[:3])
     exchange = Exchange(row, pieces, refs[3:]) if pieces else None
 
+    barrier = pltpu.get_barrier_semaphore()
+    for axis in (row, col):
+        for d in range(1, axis.n):
+            pl.semaphore_signal(barrier, inc=1, device_id={axis.name: axis.peer(d)}, device_id_type=MESH)
+    bring = [pltpu.make_async_copy(src, dst, bring_sems.at[at]) for at, (src, dst) in enumerate(
+        ((row_hbm, row_ref), (col_hbm, col_ref), (count_hbm, count_ref), (sino_hbm, sino_ref)))]
+    for copy in bring:
+        copy.start()
     slots = tiles_hbm.shape[0]
     load = pltpu.make_async_copy(tiles_hbm, tiles.at[pl.ds(0, slots)], load_sem)
     load.start()
+    for copy in bring:
+        copy.wait()
     tiles[slots] = jnp.zeros(tiles.shape[1:], tiles.dtype)
 
     place = (row_ref[...] * VT + col_ref[...]).astype(F32)
@@ -441,10 +462,6 @@
     fill = pltpu.make_async_copy(table, slot_ref, table_sem)
     fill.start()
 
-    barrier = pltpu.get_barrier_semaphore()
-    for axis in (row, col):
-        for d in range(1, axis.n):
-            pl.semaphore_signal(barrier, inc=1, device_id={axis.name: axis.peer(d)}, device_id_type=MESH)
     pl.semaphore_wait(barrier, n_row + n_col - 2)
 
     share = RT * VT // col.n_out
@@ -455,8 +472,10 @@
             fill.wait()
         build(slot_ref, tiles, dense, flipped, step * share, (step + 1) * share)
 
-    col.all_gather(sino_ref[...], rays, build_share)
-    held[...] = rays[...].astype(F32)
+    def widen(rows):
+        held[rows, :] = rays[rows, :].astype(F32)
+
+    col.all_gather(sino_ref[...], rays, build_share, widen)
     residual_ref[...] = sino_ref[...]
     volume_ref[...] = jnp.zeros_like(volume_ref)
     direction[...] = jnp.zeros_like(direction)
@@ -466,16 +485,21 @@
 
     def iteration(k, carry):
         if exchange:
-            exchange.run(flipped, rays, voxels, search)
+            settle = exchange.run(flipped, rays, voxels, search)
         else:
             search[...] = row.reduce_scatter(flipped, rays)
             row.all_gather(search[...], voxels)
+            settle = lambda: None
+
+        def queued():
+            col.norm_send(squares(voxels, 256), 0)
+            settle()
 
         @pl.when(k == 0)
         def _():
             guess[...] = row.norm_wait(1)
 
-        forth = col.reduce_scatter(dense, voxels, lambda: col.norm_send(squares(voxels, 256), 0))
+        forth = col.reduce_scatter(dense, voxels, queued)
         fresh = col.norm_wait(0)
         beta = jnp.where(k > 0, fresh / gamma[...], jnp.zeros_like(fresh))
         gamma[...] = fresh
@@ -495,9 +519,13 @@
 
         @pl.when(k + 1 < ITERS)
         def _():
-            col.all_gather(residual_ref[...] - likely * image[...], images, start)
-            held[...] += ratio[...] * (images[...].astype(F32) - held[...])
-            rays[...] = held[...].astype(BF16)
+            def use(rows):
+                value = held[rows, :]
+                value += ratio[...] * (images[rows, :].astype(F32) - value)
+                held[rows, :] = value
+                rays[rows, :] = value.astype(BF16)
+
+            col.all_gather(residual_ref[...] - likely * image[...], images, start, use)
 
         @pl.when(k + 1 == ITERS)
         def _():
@@ -546,15 +574,6 @@
     return [buffer] * 4 + [pltpu.SemaphoreType.DMA((count,))] * 6
 
 
-def finish(volume_ref, residual_ref, volume_out, residual_out, sems):
-    copies = [pltpu.make_async_copy(volume_ref, volume_out, sems.at[0]),
-              pltpu.make_async_copy(residual_ref, residual_out, sems.at[1])]
-    for copy in copies:
-        copy.start()
-    for copy in copies:
-        copy.wait()
-
-
 def local(n_row, n_col, tiles, tile_row, tile_col, tile_count, sinogram):
     tile, frames = tiles.shape[3], sinogram.shape[2]
     n_rays, n_vox = RT * tile, VT * tile
@@ -567,14 +586,11 @@
     if n_row == 2 * CORES:
         step = min(PIECE, vox_piece)
         pieces = [(at, step) for at in range(0, 2 * vox_piece, step)]
-    hbm = pl.BlockSpec(memory_space=pl.ANY)
+    hbm = pl.BlockSpec(memory_space=pltpu.HBM)
     volume, residual = pl.pallas_call(
         functools.partial(cgls_kernel, (n_row, n_col, col_in, pieces)),
-        out_shape=(
-            jax.ShapeDtypeStruct((vox_piece, frames), F32),
-            jax.ShapeDtypeStruct((ray_piece, frames), F32),
-        ),
-        in_specs=[vmem, vmem, vmem, hbm, vmem],
+        out_shape=(pltpu.VMEM((vox_piece, frames), F32), pltpu.VMEM((ray_piece, frames), F32)),
+        in_specs=[hbm] * 5,
         out_specs=(vmem, vmem),
         scratch_shapes=[
             pltpu.VMEM((slots + 1, tile, tile), BF16),
@@ -594,6 +610,11 @@
             pltpu.VMEM((RT * VT // slots, 1, slots), jnp.int32),
             pltpu.SMEM((RT * VT // slots, 1, slots), jnp.int32),
             pltpu.SemaphoreType.DMA,
+            pltpu.VMEM((1, 1), jnp.int32),
+            pltpu.VMEM((1, slots), jnp.int32),
+            pltpu.VMEM((1, slots), jnp.int32),
+            pltpu.VMEM((ray_piece, frames), F32),
+            pltpu.SemaphoreType.DMA((4,)),
         ]
         + axis_scratch(n_row, CORES, vox_piece, frames)
         + (line_scratch if n_col == 4 * col_in else axis_scratch)(n_col, col_in, ray_piece, frames)
@@ -604,17 +625,6 @@
         ),
         name="cgls",
     )(tile_count, tile_row[0], tile_col[0], tiles[0, 0], sinogram[0])
-    volume, residual = pl.pallas_call(
-        finish,
-        out_shape=(
-            jax.ShapeDtypeStruct((vox_piece, frames), F32),
-            jax.ShapeDtypeStruct((ray_piece, frames), F32),
-        ),
-        in_specs=[vmem, vmem],
-        out_specs=(hbm, hbm),
-        scratch_shapes=[pltpu.SemaphoreType.DMA((2,))],
-        name="finish",
-    )(volume, residual)
     return volume[None], residual[None]
 
 

time: 146 us -> 142 us (0.973)
  Pallas kernels: 145 us -> 139 us
    pallas_call x1, Pallas kernels: 143 us -> 139 us  [local(): pl.pallas_call(functools.partial(cgls_kernel, (n_row, n_col, col_in, piec...]
    pallas_call x1 -> x0, Pallas kernels: 1.74 us -> none  [local(): pl.pallas_call(finish, out_shape=(jax.ShapeDtypeStruct((vox_piece, frames...]
where the time goes in v2:
time: 142 us
  Pallas kernels  139 us (98%)
    pallas_call x1, Pallas kernels, local(): pl.pallas_call(functools.partial(cgls_kernel, (n_row, n_col, col_in, piec...  139 us

profile of v2, /device:TPU:0, one launch (start us, length us, event | category | flops | bytes accessed | tf_op | source)
XLA Modules:
  0.0 141.8 jit_solution(2800649815173141223)
XLA Ops:
  1.3 139.1 %cgls.1 = (f32[512,128]{1,0:T(8,128)S(1)}, f32[256,128]{1,0:T(8,128)S(1)}) custom-call(s32[1,1]{1,0:T(1,128)S(6)} %copy.11.count_hbm, s32[1,128]{1,0:T(1,128)} %bitcast.10, s32[1,128]{1,0:T(1,128)} %bitcast.11, bf16[128,128,128]{2,1,0:T(8,128)(2,1)} %bitcast.8, f32[256,128]{1,0:T(8,128)} %bitcast.9), custom_call_target="tpu_custom_call" | custom-call | tf_op jit(solution)/shard_map/cgls/pallas_call | solution.py:590
  140.4 0.7 copy.9
  141.1 0.7 copy.10

commit v3 on v2

--- a/solution.py
+++ b/solution.py
@@ -151,7 +151,7 @@
 
 class Line(Axis):
     def __init__(self, name, n, n_in, chunk, refs):
-        self.near_out, self.near_in, self.far_out, self.far_in, self.norm_in, self.hold, self.total = refs[:7]
+        self.near_out, self.near_in, self.far_out, self.far_in, self.norm_in, self.hold, self.kept = refs[:7]
         (self.near_ss, self.near_rs, self.far_ss, self.far_rs, self.out_ss, self.out_rs,
          self.in_ss, self.in_rs, self.norm_ss, self.norm_rs) = refs[7:]
         self.name, self.n, self.n_in, self.n_out, self.chunk = name, n, n_in, n // n_in, chunk
@@ -198,7 +198,7 @@
         queued()
 
         def gathered(place, h):
-            part = self.hold[self.span(h)]
+            part = self.kept[place, self.span(h)]
             for d in others:
                 self.link(self.near_out.at[d - 1, place, self.span(h)], self.near_in.at[d - 1, place, self.span(h)],
                           self.near_ss.at[d - 1, place, h], self.near_rs.at[d - 1, place, h],
@@ -210,34 +210,32 @@
             return self.link(self.far_out.at[which, self.span(h)], self.far_in.at[slot, self.span(h)],
                              self.far_ss.at[which, h], self.far_rs.at[slot, h], self.at(place))
 
-        self.hold[...] = piece(self.at(3))
-        for h in parts:
-            self.hold[self.span(h)] = gathered(3, h)
+        for place in (3, 2, 1, 0):
+            self.kept[place] = piece(self.at(place))
+        for h in parts:
+            self.kept[3, self.span(h)] = gathered(3, h)
 
             @pl.when(self.edge)
             def _():
-                self.far_out[2, self.span(h)] = self.hold[self.span(h)].astype(BF16)
+                self.far_out[2, self.span(h)] = self.kept[3, self.span(h)].astype(BF16)
                 far(2, 3, h, 1).start()
 
-        self.total[...] = self.hold[...]
-        self.hold[...] = piece(self.at(2))
         for h in parts:
             self.far_out[1, self.span(h)] = gathered(2, h).astype(BF16)
             far(1, jnp.where(self.edge, 2, 1), h, 2).start()
-        self.hold[...] = piece(self.at(1))
+
+        for h in parts:
+            self.far_out[0, self.span(h)] = gathered(1, h).astype(BF16)
+            far(0, 0, h, 1).start()
 
         @pl.when(self.inner)
         def _():
             for h in parts:
                 far(2, 3, h, 1).wait_recv()
-                value = self.total[self.span(h)] + self.far_in[3, self.span(h)].astype(F32)
+                value = self.kept[3, self.span(h)] + self.far_in[3, self.span(h)].astype(F32)
                 self.far_out[2, self.span(h)] = value.astype(BF16)
                 far(2, 1, h, 3).start()
 
-        for h in parts:
-            self.far_out[0, self.span(h)] = gathered(1, h).astype(BF16)
-            far(0, 0, h, 1).start()
-        self.hold[...] = piece(self.at(0))
         for h in parts:
             self.hold[self.span(h)] = gathered(0, h)
         for h in parts:
@@ -562,7 +560,7 @@
         pltpu.VMEM((4, chunk, frames), BF16),
         pltpu.VMEM((2, n, 1, frames), F32),
         pltpu.VMEM((chunk, frames), F32),
-        pltpu.VMEM((chunk, frames), F32),
+        pltpu.VMEM((4, chunk, frames), F32),
         dma(near + (PARTS,)), dma(near + (PARTS,)), dma((3, PARTS)), dma((4, PARTS)),
         dma((3, PARTS)), dma((3, PARTS)), dma(near + (PARTS,)), dma(near + (PARTS,)),
         dma((2, n - 1)), dma((2, n - 1)),
@@ -585,7 +583,8 @@
     pieces = []
     if n_row == 2 * CORES:
         step = min(PIECE, vox_piece)
-        pieces = [(at, step) for at in range(0, 2 * vox_piece, step)]
+        pieces = [(at, step) for at in range(0, 2 * vox_piece - step, step)]
+        pieces += [(2 * vox_piece - at, step // 2) for at in (step, step // 2)]
     hbm = pl.BlockSpec(memory_space=pltpu.HBM)
     volume, residual = pl.pallas_call(
         functools.partial(cgls_kernel, (n_row, n_col, col_in, pieces)),

time: 142 us -> 141 us (level)
  no operation moved by 1% of the time
where the time goes in v3:
time: 141 us
  Pallas kernels  138 us (98%)
    pallas_call x1, Pallas kernels, local(): pl.pallas_call(functools.partial(cgls_kernel, (n_row, n_col, col_in, piec...  138 us

profile of v3, /device:TPU:0, one launch (start us, length us, event | category | flops | bytes accessed | tf_op | source)
XLA Modules:
  0.0 140.7 jit_solution(15296273280916236866)
XLA Ops:
  1.3 138.0 %cgls.1 = (f32[512,128]{1,0:T(8,128)S(1)}, f32[256,128]{1,0:T(8,128)S(1)}) custom-call(s32[1,1]{1,0:T(1,128)S(6)} %copy.11.count_hbm, s32[1,128]{1,0:T(1,128)} %bitcast.10, s32[1,128]{1,0:T(1,128)} %bitcast.11, bf16[128,128,128]{2,1,0:T(8,128)(2,1)} %bitcast.8, f32[256,128]{1,0:T(8,128)} %bitcast.9), custom_call_target="tpu_custom_call" | custom-call | tf_op jit(solution)/shard_map/cgls/pallas_call | solution.py:589
  139.3 0.7 copy.9
  140.0 0.7 copy.10
